TPU v7x, 32 devices: a whole 2x2x4 slice. The times are simulated.
32 devices in a mesh: ep: 16 (over z, x, core), dp: 2 (over y).
Axes of the slice: x: 2, y: 2, z: 4, core: 2. Of those that a mesh axis runs over, the one named last changes fastest.
Arguments:
- tokens: bfloat16 [4096, 2048], P(('dp', 'ep')), parts along dimension 0, may hold values from -6 to 6
- expert_ids: int32 [4096, 8], P(('dp', 'ep')), parts along dimension 0, may hold values from 0 to 15, all different within a row; in each aligned block of 128 rows (0 to 127, 128 to 255, ...) at most 96 rows name the same one
- route_logits: float32 [4096, 8], P(('dp', 'ep')), parts along dimension 0, may hold values from -3 to 300
- w_gate: bfloat16 [16, 2048, 1024], P('ep'), may hold values from -0.125 to 0.125
- w_up: bfloat16 [16, 2048, 1024], P('ep'), may hold values from -0.125 to 0.125
- w_down: bfloat16 [16, 1024, 2048], P('ep'), may hold values from -0.1875 to 0.1875
Outputs:
- mixed_rows: bfloat16 [4096, 2048], P(('dp', 'ep')), parts along dimension 0
There are 2 independent parts, one for each index of `dp`. A program takes and returns all parts, laid end to end along the dimension named above; an argument that names none is the same for every part. Nothing has to cross between parts.
Inputs may be any that keep to these rules, and one draw needn't show every extreme that they name: `expert_ids`: each row names 8 different experts; among the 128 rows of one device no expert is named more than 96 times, a bound that some block reaches.
All inputs are finite; a program needn't handle non-finite values.
Results may differ from a plain program's by a relative error of at most 0.0058.
Values may be sent and summed in bfloat16 or wider, within the bound.
A program may use at most 128 MiB of HBM per device.

v0:
```python
import jax
import jax.numpy as jnp
from jax import lax
from jax.sharding import PartitionSpec as P


def expert_ffn(rows, gate_weight, up_weight, down_weight):
    gate = jnp.dot(rows, gate_weight, preferred_element_type=jnp.float32)
    up_part = jnp.dot(rows, up_weight, preferred_element_type=jnp.float32)
    hidden = (jax.nn.silu(gate) * up_part).astype(jnp.bfloat16)
    return jnp.dot(hidden, down_weight, preferred_element_type=jnp.float32).astype(jnp.bfloat16)


def blockwise(rows, live_rows, weights):
    turns = (live_rows + 127) // 128

    def step(block_index, result):
        first_row = block_index * 128
        block_rows = lax.dynamic_slice_in_dim(rows, first_row, 128, 0)
        answer = expert_ffn(block_rows, weights[0], weights[1], weights[2])
        return lax.dynamic_update_slice_in_dim(result, answer, first_row, 0)

    return lax.fori_loop(jnp.int32(0), turns, step, jnp.zeros(rows.shape, jnp.bfloat16))


def per_device(tokens, expert_ids, route_logits, w_gate, w_up, w_down):
    tok_rows, model_width = tokens.shape
    picks = expert_ids.shape[1]
    experts = lax.axis_size("ep")
    capacity = min(tok_rows, 3 * tok_rows * picks // (2 * experts))
    row_quota = tok_rows * picks
    received = experts * capacity
    spill_count = (max(received - row_quota, 128) + 127) // 128 * 128
    length = row_quota + spill_count
    flat_ids = expert_ids.reshape(-1)
    one_hot = (flat_ids[:, None] == jnp.arange(experts, dtype=jnp.int32)[None, :]).astype(jnp.int32)
    earlier = jnp.cumsum(one_hot, axis=0) - one_hot
    slot_rank = jnp.sum(earlier * one_hot, axis=1)
    counts = jnp.sum(one_hot, axis=0)
    slot_place = flat_ids * capacity + slot_rank
    source_row = jnp.arange(row_quota, dtype=jnp.int32) // picks
    slot_token = jnp.full((received,), tok_rows, jnp.int32).at[slot_place].set(source_row)
    padded_tokens = jnp.concatenate([tokens, jnp.zeros((1, model_width), tokens.dtype)], 0)
    outgoing = padded_tokens[slot_token].reshape(experts, capacity, model_width)
    all_counts = lax.all_gather(counts, "ep", axis=0, tiled=True).reshape(experts, experts)
    own_index = lax.axis_index("ep")
    from_sources = lax.dynamic_index_in_dim(all_counts, own_index, 1, keepdims=False)
    incoming = lax.all_to_all(outgoing, "ep", split_axis=0, concat_axis=0, tiled=True)
    offsets = jnp.cumsum(from_sources) - from_sources
    live_rows = jnp.sum(from_sources)
    slot_numbers = jnp.arange(capacity, dtype=jnp.int32)
    live_slot = slot_numbers[None, :] < from_sources[:, None]
    position = jnp.where(live_slot, offsets[:, None] + slot_numbers[None, :], length).reshape(-1)
    gather_order = (
        jnp.full((length,), received, jnp.int32)
        .at[position]
        .set(jnp.arange(received, dtype=jnp.int32), mode="drop")
    )
    flat_incoming = jnp.concatenate(
        [incoming.reshape(received, model_width), jnp.zeros((1, model_width), jnp.bfloat16)], 0
    )
    packed = flat_incoming[gather_order]
    own_weights = (w_gate[0], w_up[0], w_down[0])
    results = blockwise(packed, live_rows, own_weights)
    results_ext = jnp.concatenate([results, jnp.zeros((1, model_width), jnp.bfloat16)], 0)
    outgoing_back = results_ext[position].reshape(experts, capacity, model_width)
    answers = lax.all_to_all(outgoing_back, "ep", split_axis=0, concat_axis=0, tiled=True)
    mix_weights = jax.nn.softmax(route_logits, axis=-1)
    picked = answers.reshape(received, model_width)[slot_place].reshape(
        tok_rows, picks, model_width
    )
    mixed_rows = jnp.zeros((tok_rows, model_width), jnp.float32)
    for column in range(picks):
        mixed_rows = mixed_rows + mix_weights[:, column : column + 1] * picked[:, column].astype(
            jnp.float32
        )
    return mixed_rows.astype(jnp.bfloat16)


def solution(mesh):
    in_specs = (
        P(("dp", "ep"), None),
        P(("dp", "ep"), None),
        P(("dp", "ep"), None),
        P("ep", None, None),
        P("ep", None, None),
        P("ep", None, None),
    )
    out_specs = P(("dp", "ep"), None)
    return jax.shard_map(
        per_device, mesh=mesh, in_specs=in_specs, out_specs=out_specs, check_vma=False
    )
```

profile of v0, /device:TPU:11, one launch (start us, length us, event | category | flops | bytes accessed | tf_op | source)
XLA Modules:
  0.0 509.2 jit_solution(16219183412670043593)
XLA Ops:
  0.0 0.8 copy.17
  0.8 0.1 eq.29
  0.9 0.1 eq.25
  1.0 0.7 broadcast_multiply_fusion
  1.7 4.5 reduce-window.10
  6.2 0.1 slice.80
  6.3 0.1 copy.20
  6.4 0.1 copy.21
  6.5 0.1 broadcast_add_fusion
  6.6 0.1 copy.18
  6.7 0.1 mul.113
  6.8 0.1 fusion.25
  7.0 4.3 scatter_custom_fusion
  11.3 1.1 concatenate.9
  12.4 7.1 %gather_fusion = bf16[1536,2048]{1,0:T(8,128)(2,1)} fusion(bf16[129,2048]{1,0:T(8,128)(2,1)S(1)} %concatenate.9, s32[2048]{0:T(1024)S(1)} %pad_clamp_fusion.2), kind=kCustom, calls=%fused_computation | custom fusion | bytes 12589056 | tf_op jit(solution)/shard_map/gather | solution.py:44
  19.5 0.0 copy-start.1
  19.5 6.7 %all-to-all-start = ((bf16[16,96,2048]{2,1,0:T(8,128)(2,1)}), bf16[16,96,2048]{2,1,0:T(8,128)(2,1)}, u32[]{:S(2)}, u32[]{:S(2)}) async-start(bf16[16,96,2048]{2,1,0:T(8,128)(2,1)} %bitcast.88), calls=%async_computation | async-start | bytes 12582912 | tf_op jit(solution)/shard_map/all_to_all | solution.py:48
  26.1 0.0 copy-done.1
  26.2 0.6 dynamic-slice
  27.4 0.2 dynamic-update-slice
  27.6 0.1 reshape.162
  27.7 133.8 %all-reduce.4 = s32[16,16]{1,0:T(8,128)S(1)} all-reduce(s32[16,16]{1,0:T(8,128)S(1)} %reshape.162), channel_id=1, replica_groups=mesh['ep'=16,'dp'=2] {'ep'}, use_global_device_ids=true, to_apply=%add.3 | all-reduce | flops 256 | bytes 2048
  161.5 0.1 constant_dynamic-slice_fusion
  161.6 0.7 fusion.38
  163.0 0.1 add_select_fusion
  163.1 0.1 select_n.80
  163.2 6.2 %scatter_custom_fusion.1 = s32[1536]{0:T(1024)S(1)} fusion(s32[1536]{0:T(1024)S(1)} %get-tuple-element.48, s32[1536]{0:T(1024)S(1)} %iota.20, s32[]{:T(128)} %constant.79.clone.1), kind=kCustom, calls=%fused_computation.74 | custom fusion | bytes 6148 | tf_op jit(solution)/shard_map/scatter | solution.py:57
  169.5 0.0 all-to-all-done
  169.5 6.6 %concatenate.10 = bf16[1537,2048]{1,0:T(8,128)(2,1)} pad(bf16[1536,2048]{1,0:T(8,128)(2,1)} %bitcast.7, bf16[]{:T(256)} %constant.69.clone.1), padding=0_1x0_0 | pad | bytes 12587010 | tf_op jit(solution)/shard_map/concatenate | solution.py:59
  176.1 16.3 %gather_fusion.1 = bf16[1536,2048]{1,0:T(8,128)(2,1)} fusion(bf16[1537,2048]{1,0:T(8,128)(2,1)} %concatenate.10, s32[2048]{0:T(1024)S(1)} %pad_clamp_fusion.1), kind=kCustom, calls=%fused_computation.1 | custom fusion | bytes 12589056 | tf_op jit(solution)/shard_map/gather | solution.py:62
  192.4 3.4 broadcast_in_dim.14
  195.7 106.4 %while.10 = (s32[]{:T(128)}, bf16[1536,2048]{1,0:T(8,128)(2,1)}, s32[]{:T(128)}, bf16[1536,2048]{1,0:T(8,128)(2,1)}, bf16[2048,1024]{1,0:T(8,128)(2,1)}, /*index...) while((s32[]{:T(128)}, bf16[1536,2048]{1,0:T(8,128)(2,1)}, ...), condition=%wide.region_11.12_spmd, body=%wide.region_10.11_spmd.sunk | while | flops 1611661312 | bytes 15205535 | solution.py:23
  195.7 3.1 fusion.55
  198.8 5.8 %fusion.56 = bf16[1536,2048]{1,0:T(8,128)(2,1)} fusion(bf16[1536,2048]{1,0:T(8,128)(2,1)} %get-tuple-element.137, s32[]{:T(128)S(6)} %select_n.96, bf16[1024,2048]{1,0:T(8,128)(2,1)} %get-tuple-element.153, bf16[2048,1024]{1,0:T(8,128)(2,1)} %get-tuple-element.152, f32[128,1024]{1,0:T(8,128)S(1)} %fusion.55, bf16[1536,2048]{1,0:T(8,128)(2,1)} %get-tuple-element.150), kind=kOutput, calls=%fused_computation.7.clone.1 | convolution fusion | flops 1074790400 | bytes 9962496 | tf_op jit(solution)/shard_map/while/body/dot_general | solution.py:11
  204.6 3.1 fusion.55
  207.7 5.8 %fusion.56 = bf16[1536,2048]{1,0:T(8,128)(2,1)} fusion(bf16[1536,2048]{1,0:T(8,128)(2,1)} %get-tuple-element.137, s32[]{:T(128)S(6)} %select_n.96, bf16[1024,2048]{1,0:T(8,128)(2,1)} %get-tuple-element.153, bf16[2048,1024]{1,0:T(8,128)(2,1)} %get-tuple-element.152, f32[128,1024]{1,0:T(8,128)S(1)} %fusion.55, bf16[1536,2048]{1,0:T(8,128)(2,1)} %get-tuple-element.150), kind=kOutput, calls=%fused_computation.7.clone.1 | convolution fusion | flops 1074790400 | bytes 9962496 | tf_op jit(solution)/shard_map/while/body/dot_general | solution.py:11
  213.5 3.1 fusion.55
  216.6 5.8 %fusion.56 = bf16[1536,2048]{1,0:T(8,128)(2,1)} fusion(bf16[1536,2048]{1,0:T(8,128)(2,1)} %get-tuple-element.137, s32[]{:T(128)S(6)} %select_n.96, bf16[1024,2048]{1,0:T(8,128)(2,1)} %get-tuple-element.153, bf16[2048,1024]{1,0:T(8,128)(2,1)} %get-tuple-element.152, f32[128,1024]{1,0:T(8,128)S(1)} %fusion.55, bf16[1536,2048]{1,0:T(8,128)(2,1)} %get-tuple-element.150), kind=kOutput, calls=%fused_computation.7.clone.1 | convolution fusion | flops 1074790400 | bytes 9962496 | tf_op jit(solution)/shard_map/while/body/dot_general | solution.py:11
  222.4 3.1 fusion.55
  225.4 5.8 %fusion.56 = bf16[1536,2048]{1,0:T(8,128)(2,1)} fusion(bf16[1536,2048]{1,0:T(8,128)(2,1)} %get-tuple-element.137, s32[]{:T(128)S(6)} %select_n.96, bf16[1024,2048]{1,0:T(8,128)(2,1)} %get-tuple-element.153, bf16[2048,1024]{1,0:T(8,128)(2,1)} %get-tuple-element.152, f32[128,1024]{1,0:T(8,128)S(1)} %fusion.55, bf16[1536,2048]{1,0:T(8,128)(2,1)} %get-tuple-element.150), kind=kOutput, calls=%fused_computation.7.clone.1 | convolution fusion | flops 1074790400 | bytes 9962496 | tf_op jit(solution)/shard_map/while/body/dot_general | solution.py:11
  231.2 3.1 fusion.55
  234.3 5.8 %fusion.56 = bf16[1536,2048]{1,0:T(8,128)(2,1)} fusion(bf16[1536,2048]{1,0:T(8,128)(2,1)} %get-tuple-element.137, s32[]{:T(128)S(6)} %select_n.96, bf16[1024,2048]{1,0:T(8,128)(2,1)} %get-tuple-element.153, bf16[2048,1024]{1,0:T(8,128)(2,1)} %get-tuple-element.152, f32[128,1024]{1,0:T(8,128)S(1)} %fusion.55, bf16[1536,2048]{1,0:T(8,128)(2,1)} %get-tuple-element.150), kind=kOutput, calls=%fused_computation.7.clone.1 | convolution fusion | flops 1074790400 | bytes 9962496 | tf_op jit(solution)/shard_map/while/body/dot_general | solution.py:11
  240.1 3.1 fusion.55
  243.2 5.8 %fusion.56 = bf16[1536,2048]{1,0:T(8,128)(2,1)} fusion(bf16[1536,2048]{1,0:T(8,128)(2,1)} %get-tuple-element.137, s32[]{:T(128)S(6)} %select_n.96, bf16[1024,2048]{1,0:T(8,128)(2,1)} %get-tuple-element.153, bf16[2048,1024]{1,0:T(8,128)(2,1)} %get-tuple-element.152, f32[128,1024]{1,0:T(8,128)S(1)} %fusion.55, bf16[1536,2048]{1,0:T(8,128)(2,1)} %get-tuple-element.150), kind=kOutput, calls=%fused_computation.7.clone.1 | convolution fusion | flops 1074790400 | bytes 9962496 | tf_op jit(solution)/shard_map/while/body/dot_general | solution.py:11
  249.0 3.1 fusion.55
  252.1 5.8 %fusion.56 = bf16[1536,2048]{1,0:T(8,128)(2,1)} fusion(bf16[1536,2048]{1,0:T(8,128)(2,1)} %get-tuple-element.137, s32[]{:T(128)S(6)} %select_n.96, bf16[1024,2048]{1,0:T(8,128)(2,1)} %get-tuple-element.153, bf16[2048,1024]{1,0:T(8,128)(2,1)} %get-tuple-element.152, f32[128,1024]{1,0:T(8,128)S(1)} %fusion.55, bf16[1536,2048]{1,0:T(8,128)(2,1)} %get-tuple-element.150), kind=kOutput, calls=%fused_computation.7.clone.1 | convolution fusion | flops 1074790400 | bytes 9962496 | tf_op jit(solution)/shard_map/while/body/dot_general | solution.py:11
  257.8 3.1 fusion.55
  260.9 5.8 %fusion.56 = bf16[1536,2048]{1,0:T(8,128)(2,1)} fusion(bf16[1536,2048]{1,0:T(8,128)(2,1)} %get-tuple-element.137, s32[]{:T(128)S(6)} %select_n.96, bf16[1024,2048]{1,0:T(8,128)(2,1)} %get-tuple-element.153, bf16[2048,1024]{1,0:T(8,128)(2,1)} %get-tuple-element.152, f32[128,1024]{1,0:T(8,128)S(1)} %fusion.55, bf16[1536,2048]{1,0:T(8,128)(2,1)} %get-tuple-element.150), kind=kOutput, calls=%fused_computation.7.clone.1 | convolution fusion | flops 1074790400 | bytes 9962496 | tf_op jit(solution)/shard_map/while/body/dot_general | solution.py:11
  266.7 3.1 fusion.55
  269.8 5.8 %fusion.56 = bf16[1536,2048]{1,0:T(8,128)(2,1)} fusion(bf16[1536,2048]{1,0:T(8,128)(2,1)} %get-tuple-element.137, s32[]{:T(128)S(6)} %select_n.96, bf16[1024,2048]{1,0:T(8,128)(2,1)} %get-tuple-element.153, bf16[2048,1024]{1,0:T(8,128)(2,1)} %get-tuple-element.152, f32[128,1024]{1,0:T(8,128)S(1)} %fusion.55, bf16[1536,2048]{1,0:T(8,128)(2,1)} %get-tuple-element.150), kind=kOutput, calls=%fused_computation.7.clone.1 | convolution fusion | flops 1074790400 | bytes 9962496 | tf_op jit(solution)/shard_map/while/body/dot_general | solution.py:11
  275.6 3.1 fusion.55
  278.6 5.8 %fusion.56 = bf16[1536,2048]{1,0:T(8,128)(2,1)} fusion(bf16[1536,2048]{1,0:T(8,128)(2,1)} %get-tuple-element.137, s32[]{:T(128)S(6)} %select_n.96, bf16[1024,2048]{1,0:T(8,128)(2,1)} %get-tuple-element.153, bf16[2048,1024]{1,0:T(8,128)(2,1)} %get-tuple-element.152, f32[128,1024]{1,0:T(8,128)S(1)} %fusion.55, bf16[1536,2048]{1,0:T(8,128)(2,1)} %get-tuple-element.150), kind=kOutput, calls=%fused_computation.7.clone.1 | convolution fusion | flops 1074790400 | bytes 9962496 | tf_op jit(solution)/shard_map/while/body/dot_general | solution.py:11
  284.4 3.1 fusion.55
  287.5 5.8 %fusion.56 = bf16[1536,2048]{1,0:T(8,128)(2,1)} fusion(bf16[1536,2048]{1,0:T(8,128)(2,1)} %get-tuple-element.137, s32[]{:T(128)S(6)} %select_n.96, bf16[1024,2048]{1,0:T(8,128)(2,1)} %get-tuple-element.153, bf16[2048,1024]{1,0:T(8,128)(2,1)} %get-tuple-element.152, f32[128,1024]{1,0:T(8,128)S(1)} %fusion.55, bf16[1536,2048]{1,0:T(8,128)(2,1)} %get-tuple-element.150), kind=kOutput, calls=%fused_computation.7.clone.1 | convolution fusion | flops 1074790400 | bytes 9962496 | tf_op jit(solution)/shard_map/while/body/dot_general | solution.py:11
  293.3 3.1 fusion.55
  296.3 5.8 %fusion.56 = bf16[1536,2048]{1,0:T(8,128)(2,1)} fusion(bf16[1536,2048]{1,0:T(8,128)(2,1)} %get-tuple-element.137, s32[]{:T(128)S(6)} %select_n.96, bf16[1024,2048]{1,0:T(8,128)(2,1)} %get-tuple-element.153, bf16[2048,1024]{1,0:T(8,128)(2,1)} %get-tuple-element.152, f32[128,1024]{1,0:T(8,128)S(1)} %fusion.55, bf16[1536,2048]{1,0:T(8,128)(2,1)} %get-tuple-element.150), kind=kOutput, calls=%fused_computation.7.clone.1 | convolution fusion | flops 1074790400 | bytes 9962496 | tf_op jit(solution)/shard_map/while/body/dot_general | solution.py:11
  302.1 6.6 %concatenate.11 = bf16[1537,2048]{1,0:T(8,128)(2,1)} pad(bf16[1536,2048]{1,0:T(8,128)(2,1)} %get-tuple-element.43, bf16[]{:T(256)} %constant.69.clone.1), padding=0_1x0_0 | pad | bytes 12587010 | tf_op jit(solution)/shard_map/concatenate | solution.py:65
  308.7 16.3 %gather_fusion.2 = bf16[1536,2048]{1,0:T(8,128)(2,1)} fusion(bf16[1537,2048]{1,0:T(8,128)(2,1)} %concatenate.11, s32[2048]{0:T(1024)S(1)} %pad_clamp_fusion), kind=kCustom, calls=%fused_computation.2 | custom fusion | bytes 12589056 | tf_op jit(solution)/shard_map/gather | solution.py:66
  325.0 6.9 %all-to-all-start.1 = ((bf16[16,96,2048]{2,1,0:T(8,128)(2,1)}), bf16[16,96,2048]{2,1,0:T(8,128)(2,1)}, u32[]{:S(2)}, u32[]{:S(2)}) async-start(bf16[16,96,2048]{2,1,0:T(8,128)(2,1)} %bitcast.89), calls=%async_computation.1 | async-start | bytes 12582912 | tf_op jit(solution)/shard_map/all_to_all | solution.py:67
  331.9 0.0 copy-done
  332.0 137.3 %all-to-all-done.1 = bf16[16,96,2048]{2,1,0:T(8,128)(2,1)} async-done(((bf16[16,96,2048]{2,1,0:T(8,128)(2,1)}), bf16[16,96,2048]{2,1,0:T(8,128)(2,1)}, u32[]{:S(2)}, u32[]{:S(2)}) %all-to-all-start.1) | async-done | bytes 6291488 | tf_op jit(solution)/shard_map/all_to_all | solution.py:67
  469.3 12.4 %gather_fusion.3 = bf16[1024,2048]{1,0:T(8,128)(2,1)} fusion(bf16[1536,2048]{1,0:T(8,128)(2,1)} %bitcast.12, s32[1024]{0:T(1024)S(1)} %broadcast_clamp_fusion), kind=kCustom, calls=%fused_computation.3 | custom fusion | bytes 8392704 | tf_op jit(solution)/shard_map/gather | solution.py:69
  481.7 22.1 %fusion.39 = (bf16[128,1,2048]{2,1,0:T(2,128)(2,1)S(1)}, bf16[128,1,2048]{2,1,0:T(2,128)(2,1)S(1)}, bf16[128,1,2048]{2,1,0:T(2,128)(2,1)S(1)}, bf16[128,1,2048]{...) fusion(bf16[128,8,2048]{2,1,0:T(8,128)(2,1)} %bitcast.87), kind=kLoop, calls=%fused_computation.94 | loop fusion | bytes 8388608 | tf_op jit(solution)/shard_map/slice | solution.py:74
  503.8 5.4 %fusion.17 = bf16[128,2048]{1,0:T(8,128)(2,1)} fusion(bf16[128,1,2048]{2,1,0:T(2,128)(2,1)S(1)} %get-tuple-element.72, bf16[128,1,2048]{2,1,0:T(2,128)(2,1)S(1)} %get-tuple-element.66, bf16[128,1,2048]{2,1,0:T(2,128)(2,1)S(1)} %get-tuple-element.67, bf16[128,1,2048]{2,1,0:T(2,128)(2,1)S(1)} %get-tuple-element.68, ...), kind=kLoop, calls=%fused_computation.24 | loop fusion | flops 6291456 | bytes 4722688 | tf_op jit(solution)/shard_map/convert_element_type | solution.py:77
  (20 shorter events, 0.2 us)
Async XLA Ops:
  19.5 6.7 %copy-start.1 = (u32[32]{0:T(128)S(1)}, u32[32]{0:T(128)}, u32[]{:S(2)}) copy-start(u32[32]{0:T(128)} %constant.94) | copy-start | bytes 388
  19.5 150.0 %all-to-all-start = ((bf16[16,96,2048]{2,1,0:T(8,128)(2,1)}), bf16[16,96,2048]{2,1,0:T(8,128)(2,1)}, u32[]{:S(2)}, u32[]{:S(2)}) async-start(bf16[16,96,2048]{2,1,0:T(8,128)(2,1)} %bitcast.88), calls=%async_computation | async-start | bytes 12582912 | tf_op jit(solution)/shard_map/all_to_all | solution.py:48
  325.0 6.9 %copy-start = (f32[128,8]{0,1:T(8,128)S(1)}, f32[128,8]{0,1:T(8,128)}, u32[]{:S(2)}) copy-start(f32[128,8]{0,1:T(8,128)} %param.10) | copy-start | bytes 12292
  325.0 144.3 %all-to-all-start.1 = ((bf16[16,96,2048]{2,1,0:T(8,128)(2,1)}), bf16[16,96,2048]{2,1,0:T(8,128)(2,1)}, u32[]{:S(2)}, u32[]{:S(2)}) async-start(bf16[16,96,2048]{2,1,0:T(8,128)(2,1)} %bitcast.89), calls=%async_computation.1 | async-start | bytes 12582912 | tf_op jit(solution)/shard_map/all_to_all | solution.py:67
where the time goes:
time: 510 us; the launch traced here: 509 us
  waiting for transfers between devices  137 us (27%)
  blocking collectives  134 us (26%)
  matrix products  106 us (21%)
  local copies, waits for them, and re-layouts  105 us (21%)
  starting transfers between devices  13.6 us (3%)
  other arithmetic  11.8 us (2%)
    all_to_all x1, waiting for transfers between devices, per_device(): lax.all_to_all(outgoing_back, 'ep', split_axis=0, concat_axis=0, tiled=True)  137 us
    unnamed x1, blocking collectives  134 us
    dot_general x12, matrix products, expert_ffn(): jnp.dot(hidden, down_weight, preferred_element_type=jnp.float32)  69.5 us
    dot_general x12, matrix products, expert_ffn(): gate = jnp.dot(rows, gate_weight, preferred_element_type=jnp.float32)  36.8 us
    slice x1, local copies, waits for them, and re-layouts, per_device(): picked[:, column].astype(jnp.float32)  22.1 us
    gather x1, local copies, waits for them, and re-layouts, per_device(): packed = flat_incoming[gather_order]  16.3 us
    gather x1, local copies, waits for them, and re-layouts, per_device(): results_ext[position].reshape(experts, capacity, model_width)  16.3 us
    gather x1, local copies, waits for them, and re-layouts, per_device(): answers.reshape(received, model_width)[slot_place]  12.4 us
  transfers between devices with their start and end apart: 2, of which 1 were waited for; matrix products, arithmetic and copies ran while one was open for 2% of the time, Pallas kernels for 0%

commit v1 on v0

--- a/solution.py
+++ b/solution.py
@@ -1,7 +1,13 @@
+import functools
+
 import jax
 import jax.numpy as jnp
 from jax import lax
+from jax.experimental import pallas as pl
+from jax.experimental.pallas import tpu as pltpu
 from jax.sharding import PartitionSpec as P
+
+VMEM_BYTES = 63 * 1024 * 1024
 
 
 def expert_ffn(rows, gate_weight, up_weight, down_weight):
@@ -77,6 +83,386 @@
     return mixed_rows.astype(jnp.bfloat16)
 
 
+def ring_place(chip, ring):
+    column, row = chip % 2, chip // 2
+    return row + column * (ring - 1 - 2 * row)
+
+
+def chip_at(place, ring):
+    column = place // (ring // 2)
+    return 2 * (place + column * (ring - 1 - 2 * place)) + column
+
+
+def remote(src, dst, send_sem, recv_sem, target):
+    return pltpu.make_async_remote_copy(
+        src_ref=src,
+        dst_ref=dst,
+        send_sem=send_sem,
+        recv_sem=recv_sem,
+        device_id={"ep": target},
+        device_id_type=pl.DeviceIdType.MESH,
+    )
+
+
+def fused_kernel(
+    n,
+    tok_ref,
+    ids_ref,
+    logits_ref,
+    wg_hbm,
+    wu_hbm,
+    wd_hbm,
+    out_ref,
+    xs,
+    wg,
+    wu,
+    wd,
+    ps,
+    sib,
+    got_r,
+    got_l,
+    put_r,
+    put_l,
+    hid,
+    gate_rows,
+    gate_all,
+    gate_col,
+    load_sem,
+    gate_send,
+    gate_recv,
+    ag_send,
+    ag_recv,
+    pass_send,
+    pass_recv,
+    own_sem,
+    sib_send,
+    sib_recv,
+    rs_send,
+    rs_recv,
+):
+    ring = n // 2
+    far = ring // 2
+    chunks = ring - 1
+    tok_rows, width = tok_ref.shape
+    part = tok_rows // 2
+    ff = wg.shape[1]
+    picks = ids_ref.shape[1]
+    me = lax.axis_index("ep")
+    core, chip = me % 2, me // 2
+    other = 1 - core
+    place = ring_place(chip, ring)
+    right = chip_at((place + 1) % ring, ring) * 2 + core
+    left = chip_at((place + ring - 1) % ring, ring) * 2 + core
+    twin = chip * 2 + other
+
+    barrier = pltpu.get_barrier_semaphore()
+
+    def greet(step, carry):
+        pl.semaphore_signal(
+            barrier,
+            inc=1,
+            device_id={"ep": (me + step) % n},
+            device_id_type=pl.DeviceIdType.MESH,
+        )
+        return carry
+
+    lax.fori_loop(1, n, greet, 0)
+
+    own_load = pltpu.make_async_copy(tok_ref, xs.at[0, core], load_sem.at[0])
+    own_load.start()
+    weight_loads = [
+        pltpu.make_async_copy(wg_hbm.at[0], wg, load_sem.at[1]),
+        pltpu.make_async_copy(wu_hbm.at[0], wu, load_sem.at[2]),
+        pltpu.make_async_copy(wd_hbm.at[0], wd, load_sem.at[3]),
+    ]
+
+    logits = logits_ref[...]
+    powers = jnp.exp(logits - jnp.max(logits, axis=1, keepdims=True))
+    gates = powers / jnp.sum(powers, axis=1, keepdims=True)
+    ids = ids_ref[...]
+    lanes = lax.broadcasted_iota(jnp.int32, (tok_rows, 128), 1)
+    spread = jnp.zeros((tok_rows, 128), jnp.float32)
+    for pick in range(picks):
+        spread = spread + jnp.where(
+            ids[:, pick : pick + 1] == lanes, gates[:, pick : pick + 1], 0.0
+        )
+    turned = spread.T
+    for expert in range(n):
+        gate_rows[expert] = turned[expert : expert + 1, :]
+    gate_all[0] = gate_rows[me]
+
+    own_load.wait()
+    pl.semaphore_wait(barrier, n - 1)
+
+    def ag_copy(way, s):
+        hop = s // 2
+        lane, sign, target = (s % 2, -1, right) if way == 0 else (1 - s % 2, 1, left)
+        rows = pl.ds(lane * part, part)
+        return remote(
+            xs.at[(sign * hop) % ring, core, rows],
+            xs.at[(sign * (hop + 1)) % ring, core, rows],
+            ag_send.at[way, s],
+            ag_recv.at[way, s],
+            target,
+        )
+
+    def pass_copy(way, s, whose):
+        lane, sign = (s % 2, -1) if way == 0 else (1 - s % 2, 1)
+        ref = xs.at[(sign * (s // 2 + 1)) % ring, whose, pl.ds(lane * part, part)]
+        return remote(ref, ref, pass_send.at[way, s], pass_recv.at[way, s], twin)
+
+    def own_copy(whose):
+        ref = xs.at[0, whose]
+        return remote(ref, ref, own_sem.at[0], own_sem.at[1], twin)
+
+    def gate_copy(step):
+        target = (me + step) % n
+        return remote(
+            gate_rows.at[target],
+            gate_all.at[step],
+            gate_send.at[step],
+            gate_recv.at[step],
+            target,
+        )
+
+    for s in range(2):
+        for way in range(2):
+            ag_copy(way, s).start()
+    own_copy(core).start()
+    for load in weight_loads:
+        load.start()
+
+    def send_gate(step, carry):
+        gate_copy(step).start()
+        return carry
+
+    lax.fori_loop(1, n, send_gate, 0)
+
+    def ag_event(k):
+        for way in range(2):
+            ag_copy(way, k).wait_recv()
+            if k + 2 < chunks:
+                ag_copy(way, k + 2).start()
+            pass_copy(way, k, core).start()
+
+    def sib_copy(o, whose):
+        return remote(
+            ps.at[o % ring, whose],
+            sib.at[o % ring],
+            sib_send.at[o % ring],
+            sib_recv.at[o % ring],
+            twin,
+        )
+
+    def rs_copy(way, s):
+        put, got, target = (put_r, got_r, right) if way == 0 else (put_l, got_l, left)
+        return remote(
+            put.at[s], got.at[s], rs_send.at[way, s], rs_recv.at[way, s], target
+        )
+
+    joined = set()
+
+    def join(o):
+        if o % ring not in joined:
+            joined.add(o % ring)
+            sib_copy(o, core).wait_recv()
+
+    def chip_sum(o, rows):
+        return ps[o % ring, core, rows, :].astype(jnp.float32) + sib[
+            o % ring, rows, :
+        ].astype(jnp.float32)
+
+    def rs_event(way, s):
+        o = far if s == 0 else far - (s + 1) // 2
+        lane, o = (s % 2, o) if way == 0 else (1 - s % 2, -o)
+        join(o)
+        put, got = (put_r, got_r) if way == 0 else (put_l, got_l)
+        total = chip_sum(o, pl.ds(lane * part, part))
+        if s >= 2:
+            rs_copy(way, s - 2).wait_recv()
+            total = total + got[s - 2].astype(jnp.float32)
+        put[s] = total.astype(jnp.bfloat16)
+        rs_copy(way, s).start()
+
+    def arrive(o):
+        if o == 0:
+            own_copy(other).wait_recv()
+        elif o == far:
+            pass_copy(0, chunks - 1, other).wait_recv()
+            pass_copy(1, chunks - 1, other).wait_recv()
+        else:
+            for s in (2 * abs(o) - 2, 2 * abs(o) - 1):
+                pass_copy(0 if o < 0 else 1, s, other).wait_recv()
+
+    ff_tile = ff // 4
+    out_tile = width // 4
+
+    def hidden_part(slot, first, last):
+        def body(j, carry):
+            x = xs[slot].reshape(2 * tok_rows, width)
+            cols = pl.ds(pl.multiple_of(j * ff_tile, ff_tile), ff_tile)
+            gate = jnp.dot(x, wg[:, cols], preferred_element_type=jnp.float32)
+            up = jnp.dot(x, wu[:, cols], preferred_element_type=jnp.float32)
+            hid[:, cols] = (gate / (1.0 + jnp.exp(-gate)) * up).astype(jnp.bfloat16)
+            return carry
+
+        lax.fori_loop(first, last, body, 0)
+
+    def answer_part(slot):
+        def body(j, carry):
+            cols = pl.ds(pl.multiple_of(j * out_tile, out_tile), out_tile)
+            answer = jnp.dot(hid[...], wd[:, cols], preferred_element_type=jnp.float32)
+            scale = jnp.concatenate([gate_col[...]] * (out_tile // 128), axis=1)
+            ps[slot, :, :, cols] = (
+                (answer * scale).astype(jnp.bfloat16).reshape(2, tok_rows, out_tile)
+            )
+            return carry
+
+        lax.fori_loop(0, 4, body, 0)
+
+    order = [0]
+    for d in range(1, far - 1):
+        order += [-d, d]
+    order = order[:-1] + [1 - far, far, far - 1, far - 2]
+    hooks = {}
+    for k in range(chunks):
+        b = k // 2 + 1
+        step = min(order.index(-b) if b < far else ring, order.index(b))
+        hooks.setdefault(min(3 * step - 1, max(1, 7 * k // 3)), []).append(
+            functools.partial(ag_event, k)
+        )
+    last = 3 * ring
+    hooks.setdefault(last - 6, []).extend(
+        [functools.partial(rs_event, w, s) for w, s in ((0, 0), (1, 0), (1, 1))]
+    )
+    hooks.setdefault(last - 3, []).append(functools.partial(rs_event, 0, 1))
+    hooks.setdefault(last - 2, []).extend(
+        [functools.partial(rs_event, w, 2) for w in (1, 0)]
+    )
+
+    def wait_gate(step, carry):
+        gate_copy(step).wait_recv()
+        return carry
+
+    third = 0
+    for index, o in enumerate(order):
+        slot = o % ring
+        arrive(o)
+        if index == 0:
+            weight_loads[0].wait()
+            weight_loads[1].wait()
+        for piece in range(3):
+            if piece == 0:
+                hidden_part(slot, 0, 2)
+            elif piece == 1:
+                hidden_part(slot, 2, 4)
+            else:
+                if index == 0:
+                    weight_loads[2].wait()
+                    lax.fori_loop(1, n, wait_gate, 0)
+                for whose in range(2):
+                    source = chip_at((place + slot) % ring, ring) * 2 + whose
+                    row = gate_all[(me + n - source) % n]
+                    gate_col[pl.ds(whose * tok_rows, tok_rows), :] = jnp.broadcast_to(
+                        row, (128, tok_rows)
+                    ).T
+                answer_part(slot)
+                sib_copy(o, other).start()
+            for hook in hooks.get(third, []):
+                hook()
+            third += 1
+
+    for s in range(3, chunks):
+        for way in (1, 0):
+            rs_event(way, s)
+    join(0)
+    for lane in (1, 0):
+        rows = pl.ds(lane * part, part)
+        s_right, s_left = (chunks - 2, chunks - 1) if lane == 1 else (chunks - 1, chunks - 2)
+        if lane == 1:
+            for s in (chunks - 2, chunks - 1):
+                for way in range(2):
+                    rs_copy(way, s).wait_recv()
+        total = chip_sum(0, rows)
+        total = total + got_r[s_right].astype(jnp.float32)
+        total = total + got_l[s_left].astype(jnp.float32)
+        out_ref[rows, :] = total.astype(jnp.bfloat16)
+    for s in range(chunks):
+        for way in range(2):
+            ag_copy(way, s).wait_send()
+            pass_copy(way, s, core).wait_send()
+            rs_copy(way, s).wait_send()
+    for o in range(ring):
+        join(o)
+        sib_copy(o, other).wait_send()
+    own_copy(core).wait_send()
+
+    def drain_gate(step, carry):
+        gate_copy(step).wait_send()
+        return carry
+
+    lax.fori_loop(1, n, drain_gate, 0)
+
+
+def fused_scratch(n, tok_rows, width, ff):
+    ring = n // 2
+    chunks, part, bf16 = ring - 1, tok_rows // 2, jnp.bfloat16
+    buffers = [
+        ((ring, 2, tok_rows, width), bf16),
+        ((width, ff), bf16),
+        ((width, ff), bf16),
+        ((ff, width), bf16),
+        ((ring, 2, tok_rows, width), bf16),
+        ((ring, tok_rows, width), bf16),
+        ((chunks, part, width), bf16),
+        ((chunks, part, width), bf16),
+        ((chunks, part, width), bf16),
+        ((chunks, part, width), bf16),
+        ((2 * tok_rows, ff), bf16),
+        ((n, 1, tok_rows), jnp.float32),
+        ((n, 1, tok_rows), jnp.float32),
+        ((2 * tok_rows, 128), jnp.float32),
+    ]
+    sems = [(4,), (n,), (n,), (2, chunks), (2, chunks), (2, chunks), (2, chunks), (2,), (ring,), (ring,), (2, chunks), (2, chunks)]
+    size = 0
+    for shape, kind in buffers:
+        count = jnp.dtype(kind).itemsize
+        for extent in shape:
+            count = count * extent
+        size = size + count
+    scratch = [pltpu.VMEM(shape, kind) for shape, kind in buffers]
+    return scratch + [pltpu.SemaphoreType.DMA(shape) for shape in sems], size
+
+
+def fused_device(tokens, expert_ids, route_logits, w_gate, w_up, w_down):
+    n = lax.axis_size("ep")
+    tok_rows, width = tokens.shape
+    ff = w_gate.shape[2]
+    scratch, size = fused_scratch(n, tok_rows, width, ff)
+    anywhere, vmem = pl.BlockSpec(memory_space=pl.ANY), pl.BlockSpec(memory_space=pltpu.VMEM)
+    return pl.pallas_call(
+        functools.partial(fused_kernel, n),
+        out_shape=jax.ShapeDtypeStruct((tok_rows, width), jnp.bfloat16),
+        in_specs=[anywhere, vmem, vmem, anywhere, anywhere, anywhere],
+        out_specs=vmem,
+        scratch_shapes=scratch,
+        compiler_params=pltpu.CompilerParams(
+            collective_id=0, has_side_effects=True, vmem_limit_bytes=VMEM_BYTES
+        ),
+    )(tokens, expert_ids, route_logits, w_gate, w_up, w_down)
+
+
+def layer(tokens, expert_ids, route_logits, w_gate, w_up, w_down):
+    n = lax.axis_size("ep")
+    tok_rows, width = tokens.shape
+    ff = w_gate.shape[2]
+    size = fused_scratch(n, tok_rows, width, ff)[1]
+    fits = size + 8 * tok_rows * width < VMEM_BYTES
+    if fits and n % 4 == 0 and n >= 12 and tok_rows == 128 and n <= 128:
+        return fused_device(tokens, expert_ids, route_logits, w_gate, w_up, w_down)
+    return per_device(tokens, expert_ids, route_logits, w_gate, w_up, w_down)
+
+
 def solution(mesh):
     in_specs = (
         P(("dp", "ep"), None),
@@ -88,5 +474,5 @@
     )
     out_specs = P(("dp", "ep"), None)
     return jax.shard_map(
-        per_device, mesh=mesh, in_specs=in_specs, out_specs=out_specs, check_vma=False
-    )
+        layer, mesh=mesh, in_specs=in_specs, out_specs=out_specs, check_vma=False
+    )

time: 510 us -> 108 us (0.21)
  the two profiles are of different devices: /device:TPU:11 before, /device:TPU:0 now
where the time goes in v1:
time: 108 us; the launch traced here: 107 us
  Pallas kernels  103 us (95%)
  local copies, waits for them, and re-layouts  4.7 us (4%)
    pallas_call x1, Pallas kernels, fused_device(): pl.pallas_call(functools.partial(fused_kernel, n), out_shape=jax.ShapeDty...  103 us
    unnamed x3, local copies, waits for them, and re-layouts  4.7 us

profile of v1, /device:TPU:0, one launch (start us, length us, event | category | flops | bytes accessed | tf_op | source)
XLA Modules:
  0.0 107.2 jit_solution(17534509503077744546)
XLA Ops:
  0.0 1.4 %copy.7.ids_ref = s32[128,8]{1,0:T(8,128)} copy(s32[128,8]{0,1:T(8,128)} %param.7) | data formatting | bytes 8192 | tf_op args[1]
  1.4 1.4 %copy.8.logits_ref = f32[128,8]{1,0:T(8,128)} copy(f32[128,8]{0,1:T(8,128)} %param.8) | data formatting | bytes 8192 | tf_op args[2]
  2.8 102.5 %shard_map.64 = bf16[128,2048]{1,0:T(8,128)(2,1)} custom-call(bf16[128,2048]{1,0:T(8,128)(2,1)} %tok_ref.1, s32[128,8]{1,0:T(8,128)} %copy.7.ids_ref, f32[128,8]{1,0:T(8,128)} %copy.8.logits_ref, bf16[1,2048,1024]{2,1,0:T(8,128)(2,1)} %wg_hbm.1, bf16[1,2048,1024]{2,1,0:T(8,128)(2,1)} %wu_hbm.1, bf16[1,1024,2048]{2,1,0:T(8,128)(2,1)} %wd_hbm.1), custom_call_target="tpu_custom_call" | custom-call | tf_op jit(solution)/shard_map/pallas_call | solution.py:443
  105.4 1.9 %copy.10 = bf16[128,2048]{1,0:T(8,128)(2,1)} copy(bf16[128,2048]{1,0:T(8,128)(2,1)} %shard_map.64) | data formatting | bytes 1048576

commit v2 on v1

--- a/solution.py
+++ b/solution.py
@@ -141,12 +141,10 @@
     rs_recv,
 ):
     ring = n // 2
-    far = ring // 2
     chunks = ring - 1
     tok_rows, width = tok_ref.shape
     part = tok_rows // 2
     ff = wg.shape[1]
-    picks = ids_ref.shape[1]
     me = lax.axis_index("ep")
     core, chip = me % 2, me // 2
     other = 1 - core
@@ -177,38 +175,32 @@
     ]
 
     logits = logits_ref[...]
-    powers = jnp.exp(logits - jnp.max(logits, axis=1, keepdims=True))
-    gates = powers / jnp.sum(powers, axis=1, keepdims=True)
+    powers = jnp.exp(logits - jnp.max(logits, axis=0, keepdims=True))
+    gates = powers / jnp.sum(powers, axis=0, keepdims=True)
     ids = ids_ref[...]
-    lanes = lax.broadcasted_iota(jnp.int32, (tok_rows, 128), 1)
-    spread = jnp.zeros((tok_rows, 128), jnp.float32)
-    for pick in range(picks):
-        spread = spread + jnp.where(
-            ids[:, pick : pick + 1] == lanes, gates[:, pick : pick + 1], 0.0
-        )
-    turned = spread.T
     for expert in range(n):
-        gate_rows[expert] = turned[expert : expert + 1, :]
+        gate_rows[expert] = jnp.sum(
+            jnp.where(ids == expert, gates, 0.0), axis=0, keepdims=True
+        )
     gate_all[0] = gate_rows[me]
 
     own_load.wait()
     pl.semaphore_wait(barrier, n - 1)
 
     def ag_copy(way, s):
-        hop = s // 2
-        lane, sign, target = (s % 2, -1, right) if way == 0 else (1 - s % 2, 1, left)
-        rows = pl.ds(lane * part, part)
+        target = right if way == 0 else left
+        rows = pl.ds(way * part, part)
+        if s < 2:
+            lane = s if way == 0 else 1 - s
+            src = xs.at[0, core, pl.ds(lane * part, part)]
+        else:
+            src = xs.at[s - 1, core, rows]
         return remote(
-            xs.at[(sign * hop) % ring, core, rows],
-            xs.at[(sign * (hop + 1)) % ring, core, rows],
-            ag_send.at[way, s],
-            ag_recv.at[way, s],
-            target,
+            src, xs.at[s + 1, core, rows], ag_send.at[way, s], ag_recv.at[way, s], target
         )
 
     def pass_copy(way, s, whose):
-        lane, sign = (s % 2, -1) if way == 0 else (1 - s % 2, 1)
-        ref = xs.at[(sign * (s // 2 + 1)) % ring, whose, pl.ds(lane * part, part)]
+        ref = xs.at[s + 1, whose, pl.ds(way * part, part)]
         return remote(ref, ref, pass_send.at[way, s], pass_recv.at[way, s], twin)
 
     def own_copy(whose):
@@ -245,54 +237,41 @@
                 ag_copy(way, k + 2).start()
             pass_copy(way, k, core).start()
 
-    def sib_copy(o, whose):
+    def sib_copy(slot, whose):
         return remote(
-            ps.at[o % ring, whose],
-            sib.at[o % ring],
-            sib_send.at[o % ring],
-            sib_recv.at[o % ring],
-            twin,
-        )
-
-    def rs_copy(way, s):
+            ps.at[slot, whose], sib.at[slot], sib_send.at[slot], sib_recv.at[slot], twin
+        )
+
+    def rs_copy(way, k):
         put, got, target = (put_r, got_r, right) if way == 0 else (put_l, got_l, left)
         return remote(
-            put.at[s], got.at[s], rs_send.at[way, s], rs_recv.at[way, s], target
-        )
-
-    joined = set()
-
-    def join(o):
-        if o % ring not in joined:
-            joined.add(o % ring)
-            sib_copy(o, core).wait_recv()
-
-    def chip_sum(o, rows):
-        return ps[o % ring, core, rows, :].astype(jnp.float32) + sib[
-            o % ring, rows, :
-        ].astype(jnp.float32)
-
-    def rs_event(way, s):
-        o = far if s == 0 else far - (s + 1) // 2
-        lane, o = (s % 2, o) if way == 0 else (1 - s % 2, -o)
-        join(o)
-        put, got = (put_r, got_r) if way == 0 else (put_l, got_l)
-        total = chip_sum(o, pl.ds(lane * part, part))
-        if s >= 2:
-            rs_copy(way, s - 2).wait_recv()
-            total = total + got[s - 2].astype(jnp.float32)
-        put[s] = total.astype(jnp.bfloat16)
-        rs_copy(way, s).start()
-
-    def arrive(o):
-        if o == 0:
+            put.at[k], got.at[k], rs_send.at[way, k], rs_recv.at[way, k], target
+        )
+
+    def chip_sum(slot, rows):
+        return ps[slot, core, rows, :].astype(jnp.float32) + sib[slot, rows, :].astype(
+            jnp.float32
+        )
+
+    def rs_event(k):
+        sib_copy(k + 1, core).wait_recv()
+        for way in range(2):
+            put, got = (put_r, got_r) if way == 0 else (put_l, got_l)
+            side = way if k == chunks - 1 else 1 - way
+            total = chip_sum(k + 1, pl.ds(side * part, part))
+            if k not in (chunks - 1, chunks - 3):
+                before = chunks - 1 if k == chunks - 2 else k + 2
+                rs_copy(way, before).wait_recv()
+                total = total + got[before].astype(jnp.float32)
+            put[k] = total.astype(jnp.bfloat16)
+            rs_copy(way, k).start()
+
+    def arrive(slot):
+        if slot == 0:
             own_copy(other).wait_recv()
-        elif o == far:
-            pass_copy(0, chunks - 1, other).wait_recv()
-            pass_copy(1, chunks - 1, other).wait_recv()
         else:
-            for s in (2 * abs(o) - 2, 2 * abs(o) - 1):
-                pass_copy(0 if o < 0 else 1, s, other).wait_recv()
+            for way in range(2):
+                pass_copy(way, slot - 1, other).wait_recv()
 
     ff_tile = ff // 4
     out_tile = width // 4
@@ -320,34 +299,28 @@
 
         lax.fori_loop(0, 4, body, 0)
 
-    order = [0]
-    for d in range(1, far - 1):
-        order += [-d, d]
-    order = order[:-1] + [1 - far, far, far - 1, far - 2]
+    order = [0] + [k + 1 for k in range(chunks - 4)]
+    order += [chunks - 2, chunks, chunks - 1, chunks - 3]
+    last = 3 * ring
     hooks = {}
     for k in range(chunks):
-        b = k // 2 + 1
-        step = min(order.index(-b) if b < far else ring, order.index(b))
-        hooks.setdefault(min(3 * step - 1, max(1, 7 * k // 3)), []).append(
+        due = min(3 * order.index(later + 1) - 1 for later in range(k, chunks))
+        hooks.setdefault(min(due, 5 * k // 2 + 1), []).append(
             functools.partial(ag_event, k)
         )
-    last = 3 * ring
-    hooks.setdefault(last - 6, []).extend(
-        [functools.partial(rs_event, w, s) for w, s in ((0, 0), (1, 0), (1, 1))]
-    )
-    hooks.setdefault(last - 3, []).append(functools.partial(rs_event, 0, 1))
-    hooks.setdefault(last - 2, []).extend(
-        [functools.partial(rs_event, w, 2) for w in (1, 0)]
-    )
+    firsts, seconds = list(range(chunks - 3, -1, -2)), [chunks - 1]
+    seconds += list(range(chunks - 2, 0, -2))
+    sends = [k for pair in zip(firsts, seconds) for k in pair] + seconds[len(firsts) :]
+    for third, k in zip((last - 10, last - 6, last - 5, last - 2), sends):
+        hooks.setdefault(third, []).append(functools.partial(rs_event, k))
 
     def wait_gate(step, carry):
         gate_copy(step).wait_recv()
         return carry
 
     third = 0
-    for index, o in enumerate(order):
-        slot = o % ring
-        arrive(o)
+    for index, slot in enumerate(order):
+        arrive(slot)
         if index == 0:
             weight_loads[0].wait()
             weight_loads[1].wait()
@@ -360,41 +333,42 @@
                 if index == 0:
                     weight_loads[2].wait()
                     lax.fori_loop(1, n, wait_gate, 0)
-                for whose in range(2):
-                    source = chip_at((place + slot) % ring, ring) * 2 + whose
-                    row = gate_all[(me + n - source) % n]
-                    gate_col[pl.ds(whose * tok_rows, tok_rows), :] = jnp.broadcast_to(
-                        row, (128, tok_rows)
-                    ).T
+                for way in range(2):
+                    hop = (slot + 1) // 2
+                    lane = (slot + 1 + way) % 2 if slot > 0 else way
+                    where = place - hop if way == 0 else place + hop
+                    spot = chip_at((where + ring) % ring, ring) * 2
+                    for whose in range(2):
+                        row = gate_all[(me + n - spot - whose) % n]
+                        gate_col[pl.ds(whose * tok_rows + way * part, part), :] = (
+                            jnp.broadcast_to(row, (128, tok_rows)).T[
+                                lane * part : (lane + 1) * part
+                            ]
+                        )
                 answer_part(slot)
-                sib_copy(o, other).start()
+                sib_copy(slot, other).start()
             for hook in hooks.get(third, []):
                 hook()
             third += 1
 
-    for s in range(3, chunks):
-        for way in (1, 0):
-            rs_event(way, s)
-    join(0)
+    for k in sends[4:]:
+        rs_event(k)
+    sib_copy(0, core).wait_recv()
     for lane in (1, 0):
         rows = pl.ds(lane * part, part)
-        s_right, s_left = (chunks - 2, chunks - 1) if lane == 1 else (chunks - 1, chunks - 2)
-        if lane == 1:
-            for s in (chunks - 2, chunks - 1):
-                for way in range(2):
-                    rs_copy(way, s).wait_recv()
         total = chip_sum(0, rows)
-        total = total + got_r[s_right].astype(jnp.float32)
-        total = total + got_l[s_left].astype(jnp.float32)
+        for way, got in ((0, got_r), (1, got_l)):
+            k = 1 if lane == way else 0
+            rs_copy(way, k).wait_recv()
+            total = total + got[k].astype(jnp.float32)
         out_ref[rows, :] = total.astype(jnp.bfloat16)
     for s in range(chunks):
         for way in range(2):
             ag_copy(way, s).wait_send()
             pass_copy(way, s, core).wait_send()
             rs_copy(way, s).wait_send()
-    for o in range(ring):
-        join(o)
-        sib_copy(o, other).wait_send()
+    for slot in range(ring):
+        sib_copy(slot, other).wait_send()
     own_copy(core).wait_send()
 
     def drain_gate(step, carry):
@@ -449,7 +423,7 @@
         compiler_params=pltpu.CompilerParams(
             collective_id=0, has_side_effects=True, vmem_limit_bytes=VMEM_BYTES
         ),
-    )(tokens, expert_ids, route_logits, w_gate, w_up, w_down)
+    )(tokens, expert_ids.T, route_logits.T, w_gate, w_up, w_down)
 
 
 def layer(tokens, expert_ids, route_logits, w_gate, w_up, w_down):
@@ -458,7 +432,7 @@
     ff = w_gate.shape[2]
     size = fused_scratch(n, tok_rows, width, ff)[1]
     fits = size + 8 * tok_rows * width < VMEM_BYTES
-    if fits and n % 4 == 0 and n >= 12 and tok_rows == 128 and n <= 128:
+    if fits and n % 4 == 0 and n >= 16 and tok_rows == 128 and n <= 128:
         return fused_device(tokens, expert_ids, route_logits, w_gate, w_up, w_down)
     return per_device(tokens, expert_ids, route_logits, w_gate, w_up, w_down)
 

time: 108 us -> 99.1 us (0.918)
  Pallas kernels: 103 us -> 96.9 us
  local copies, waits for them, and re-layouts: 4.7 us -> 1.88 us
    pallas_call x1, Pallas kernels: 103 us -> 96.9 us  [fused_device(): pl.pallas_call(functools.partial(fused_kernel, n), out_shape=jax.ShapeDty...]
    unnamed x3 -> x1, local copies, waits for them, and re-layouts: 4.7 us -> 1.88 us
where the time goes in v2:
time: 99.1 us; the launch traced here: 98.8 us
  Pallas kernels  96.9 us (98%)
  local copies, waits for them, and re-layouts  1.88 us (2%)
    pallas_call x1, Pallas kernels, fused_device(): pl.pallas_call(functools.partial(fused_kernel, n), out_shape=jax.ShapeDty...  96.9 us

profile of v2, /device:TPU:0, one launch (start us, length us, event | category | flops | bytes accessed | tf_op | source)
XLA Modules:
  0.0 98.8 jit_solution(4624010363609889321)
XLA Ops:
  0.0 96.9 %shard_map.64 = bf16[128,2048]{1,0:T(8,128)(2,1)} custom-call(bf16[128,2048]{1,0:T(8,128)(2,1)} %tok_ref.1, s32[8,128]{1,0:T(8,128)} %bitcast.2, f32[8,128]{1,0:T(8,128)} %bitcast.3, bf16[1,2048,1024]{2,1,0:T(8,128)(2,1)} %wg_hbm.1, bf16[1,2048,1024]{2,1,0:T(8,128)(2,1)} %wu_hbm.1, bf16[1,1024,2048]{2,1,0:T(8,128)(2,1)} %wd_hbm.1), custom_call_target="tpu_custom_call" | custom-call | tf_op jit(solution)/shard_map/pallas_call | solution.py:417
  96.9 1.9 %copy.8 = bf16[128,2048]{1,0:T(8,128)(2,1)} copy(bf16[128,2048]{1,0:T(8,128)(2,1)} %shard_map.64) | data formatting | bytes 1048576

commit v3 on v2

--- a/solution.py
+++ b/solution.py
@@ -130,6 +130,8 @@
     load_sem,
     gate_send,
     gate_recv,
+    gate_out,
+    gate_in,
     ag_send,
     ag_recv,
     pass_send,
@@ -141,6 +143,7 @@
     rs_recv,
 ):
     ring = n // 2
+    far = ring // 2
     chunks = ring - 1
     tok_rows, width = tok_ref.shape
     part = tok_rows // 2
@@ -155,16 +158,13 @@
 
     barrier = pltpu.get_barrier_semaphore()
 
-    def greet(step, carry):
+    for friend in (right, left, twin):
         pl.semaphore_signal(
             barrier,
             inc=1,
-            device_id={"ep": (me + step) % n},
+            device_id={"ep": friend},
             device_id_type=pl.DeviceIdType.MESH,
         )
-        return carry
-
-    lax.fori_loop(1, n, greet, 0)
 
     own_load = pltpu.make_async_copy(tok_ref, xs.at[0, core], load_sem.at[0])
     own_load.start()
@@ -173,19 +173,20 @@
         pltpu.make_async_copy(wu_hbm.at[0], wu, load_sem.at[2]),
         pltpu.make_async_copy(wd_hbm.at[0], wd, load_sem.at[3]),
     ]
+    for load in weight_loads:
+        load.start()
 
     logits = logits_ref[...]
     powers = jnp.exp(logits - jnp.max(logits, axis=0, keepdims=True))
     gates = powers / jnp.sum(powers, axis=0, keepdims=True)
     ids = ids_ref[...]
     for expert in range(n):
-        gate_rows[expert] = jnp.sum(
+        gate_rows[core, expert] = jnp.sum(
             jnp.where(ids == expert, gates, 0.0), axis=0, keepdims=True
         )
-    gate_all[0] = gate_rows[me]
 
     own_load.wait()
-    pl.semaphore_wait(barrier, n - 1)
+    pl.semaphore_wait(barrier, 3)
 
     def ag_copy(way, s):
         target = right if way == 0 else left
@@ -207,35 +208,52 @@
         ref = xs.at[0, whose]
         return remote(ref, ref, own_sem.at[0], own_sem.at[1], twin)
 
-    def gate_copy(step):
-        target = (me + step) % n
+    def own_gate(whose):
+        ref = gate_rows.at[whose]
+        return remote(ref, ref, own_sem.at[2], own_sem.at[3], twin)
+
+    def gate_copy(way, hop):
         return remote(
-            gate_rows.at[target],
-            gate_all.at[step],
-            gate_send.at[step],
-            gate_recv.at[step],
-            target,
-        )
-
-    for s in range(2):
-        for way in range(2):
-            ag_copy(way, s).start()
+            gate_rows.at[core] if hop == 1 else gate_all.at[way, hop - 2, core],
+            gate_all.at[way, hop - 1, core],
+            gate_send.at[way, hop - 1],
+            gate_recv.at[way, hop - 1],
+            right if way == 0 else left,
+        )
+
+    def gate_pass(way, hop, whose):
+        ref = gate_all.at[way, hop - 1, whose]
+        return remote(
+            ref, ref, gate_out.at[way, hop - 1], gate_in.at[way, hop - 1], twin
+        )
+
+    for way in range(2):
+        ag_copy(way, 0).start()
+    for way in range(2):
+        ag_copy(way, 1).start()
+        gate_copy(way, 1).start()
     own_copy(core).start()
-    for load in weight_loads:
-        load.start()
-
-    def send_gate(step, carry):
-        gate_copy(step).start()
-        return carry
-
-    lax.fori_loop(1, n, send_gate, 0)
+    own_gate(core).start()
+
+    turns = list(range(chunks - 4)) + [chunks - 3, chunks - 4, chunks - 1, chunks - 2]
+    waiting, seen = [s for s in turns if s >= 2], set()
 
     def ag_event(k):
+        seen.add(k)
+        ready = []
+        while waiting and waiting[0] - 2 in seen:
+            ready.append(waiting.pop(0))
         for way in range(2):
             ag_copy(way, k).wait_recv()
-            if k + 2 < chunks:
-                ag_copy(way, k + 2).start()
+            for s in ready:
+                ag_copy(way, s).start()
             pass_copy(way, k, core).start()
+            if k % 2 == 0:
+                hop = k // 2 + 1
+                gate_copy(way, hop).wait_recv()
+                if hop < far:
+                    gate_copy(way, hop + 1).start()
+                gate_pass(way, hop, core).start()
 
     def sib_copy(slot, whose):
         return remote(
@@ -269,9 +287,12 @@
     def arrive(slot):
         if slot == 0:
             own_copy(other).wait_recv()
+            own_gate(other).wait_recv()
         else:
             for way in range(2):
                 pass_copy(way, slot - 1, other).wait_recv()
+                if slot % 2 == 1:
+                    gate_pass(way, (slot + 1) // 2, other).wait_recv()
 
     ff_tile = ff // 4
     out_tile = width // 4
@@ -303,20 +324,15 @@
     order += [chunks - 2, chunks, chunks - 1, chunks - 3]
     last = 3 * ring
     hooks = {}
-    for k in range(chunks):
-        due = min(3 * order.index(later + 1) - 1 for later in range(k, chunks))
-        hooks.setdefault(min(due, 5 * k // 2 + 1), []).append(
-            functools.partial(ag_event, k)
-        )
+    times = [(5 * i + 1) // 2 + 1 for i in range(chunks - 4)]
+    times += [last - 14, last - 12, last - 10, last - 7]
+    for time, k in zip(times, turns):
+        hooks.setdefault(time, []).append(functools.partial(ag_event, k))
     firsts, seconds = list(range(chunks - 3, -1, -2)), [chunks - 1]
     seconds += list(range(chunks - 2, 0, -2))
     sends = [k for pair in zip(firsts, seconds) for k in pair] + seconds[len(firsts) :]
     for third, k in zip((last - 10, last - 6, last - 5, last - 2), sends):
         hooks.setdefault(third, []).append(functools.partial(rs_event, k))
-
-    def wait_gate(step, carry):
-        gate_copy(step).wait_recv()
-        return carry
 
     third = 0
     for index, slot in enumerate(order):
@@ -332,14 +348,14 @@
             else:
                 if index == 0:
                     weight_loads[2].wait()
-                    lax.fori_loop(1, n, wait_gate, 0)
                 for way in range(2):
                     hop = (slot + 1) // 2
                     lane = (slot + 1 + way) % 2 if slot > 0 else way
-                    where = place - hop if way == 0 else place + hop
-                    spot = chip_at((where + ring) % ring, ring) * 2
                     for whose in range(2):
-                        row = gate_all[(me + n - spot - whose) % n]
+                        if hop == 0:
+                            row = gate_rows[whose, me]
+                        else:
+                            row = gate_all[way, hop - 1, whose, me]
                         gate_col[pl.ds(whose * tok_rows + way * part, part), :] = (
                             jnp.broadcast_to(row, (128, tok_rows)).T[
                                 lane * part : (lane + 1) * part
@@ -370,12 +386,11 @@
     for slot in range(ring):
         sib_copy(slot, other).wait_send()
     own_copy(core).wait_send()
-
-    def drain_gate(step, carry):
-        gate_copy(step).wait_send()
-        return carry
-
-    lax.fori_loop(1, n, drain_gate, 0)
+    own_gate(core).wait_send()
+    for hop in range(1, far + 1):
+        for way in range(2):
+            gate_copy(way, hop).wait_send()
+            gate_pass(way, hop, core).wait_send()
 
 
 def fused_scratch(n, tok_rows, width, ff):
@@ -393,11 +408,13 @@
         ((chunks, part, width), bf16),
         ((chunks, part, width), bf16),
         ((2 * tok_rows, ff), bf16),
-        ((n, 1, tok_rows), jnp.float32),
-        ((n, 1, tok_rows), jnp.float32),
+        ((2, n, 1, tok_rows), jnp.float32),
+        ((2, ring // 2, 2, n, 1, tok_rows), jnp.float32),
         ((2 * tok_rows, 128), jnp.float32),
     ]
-    sems = [(4,), (n,), (n,), (2, chunks), (2, chunks), (2, chunks), (2, chunks), (2,), (ring,), (ring,), (2, chunks), (2, chunks)]
+    hops, moves = (2, ring // 2), (2, chunks)
+    sems = [(4,), hops, hops, hops, hops, moves, moves, moves, moves, (4,)]
+    sems += [(ring,), (ring,), moves, moves]
     size = 0
     for shape, kind in buffers:
         count = jnp.dtype(kind).itemsize

time: 99.1 us -> 101 us (1.019)
  Pallas kernels: 96.9 us -> 98.5 us
    pallas_call x1, Pallas kernels: 96.9 us -> 98.5 us  [fused_device(): pl.pallas_call(functools.partial(fused_kernel, n), out_shape=jax.ShapeDty...]
where the time goes in v3:
time: 101 us; the launch traced here: 100 us
  Pallas kernels  98.5 us (98%)
  local copies, waits for them, and re-layouts  1.88 us (2%)
    pallas_call x1, Pallas kernels, fused_device(): pl.pallas_call(functools.partial(fused_kernel, n), out_shape=jax.ShapeDty...  98.5 us

profile of v3, /device:TPU:0, one launch (start us, length us, event | category | flops | bytes accessed | tf_op | source)
XLA Modules:
  0.0 100.4 jit_solution(5759277853435650227)
XLA Ops:
  0.0 98.5 %shard_map.64 = bf16[128,2048]{1,0:T(8,128)(2,1)} custom-call(bf16[128,2048]{1,0:T(8,128)(2,1)} %tok_ref.1, s32[8,128]{1,0:T(8,128)} %bitcast.2, f32[8,128]{1,0:T(8,128)} %bitcast.3, bf16[1,2048,1024]{2,1,0:T(8,128)(2,1)} %wg_hbm.1, bf16[1,2048,1024]{2,1,0:T(8,128)(2,1)} %wu_hbm.1, bf16[1,1024,2048]{2,1,0:T(8,128)(2,1)} %wd_hbm.1), custom_call_target="tpu_custom_call" | custom-call | tf_op jit(solution)/shard_map/pallas_call | solution.py:434
  98.5 1.9 %copy.8 = bf16[128,2048]{1,0:T(8,128)(2,1)} copy(bf16[128,2048]{1,0:T(8,128)(2,1)} %shard_map.64) | data formatting | bytes 1048576

commit v4 on v3

--- a/solution.py
+++ b/solution.py
@@ -228,10 +228,10 @@
         )
 
     for way in range(2):
+        gate_copy(way, 1).start()
         ag_copy(way, 0).start()
     for way in range(2):
         ag_copy(way, 1).start()
-        gate_copy(way, 1).start()
     own_copy(core).start()
     own_gate(core).start()
 
@@ -244,15 +244,16 @@
         while waiting and waiting[0] - 2 in seen:
             ready.append(waiting.pop(0))
         for way in range(2):
+            hop = k // 2 + 1
+            if k % 2 == 0:
+                gate_copy(way, hop).wait_recv()
+                if hop < far:
+                    gate_copy(way, hop + 1).start()
             ag_copy(way, k).wait_recv()
             for s in ready:
                 ag_copy(way, s).start()
             pass_copy(way, k, core).start()
             if k % 2 == 0:
-                hop = k // 2 + 1
-                gate_copy(way, hop).wait_recv()
-                if hop < far:
-                    gate_copy(way, hop + 1).start()
                 gate_pass(way, hop, core).start()
 
     def sib_copy(slot, whose):

time: 101 us -> 93.7 us (0.928)
  Pallas kernels: 98.5 us -> 91.7 us
    pallas_call x1, Pallas kernels: 98.5 us -> 91.7 us  [fused_device(): pl.pallas_call(functools.partial(fused_kernel, n), out_shape=jax.ShapeDty...]
where the time goes in v4:
time: 93.7 us; the launch traced here: 93.5 us
  Pallas kernels  91.7 us (98%)
  local copies, waits for them, and re-layouts  1.88 us (2%)
    pallas_call x1, Pallas kernels, fused_device(): pl.pallas_call(functools.partial(fused_kernel, n), out_shape=jax.ShapeDty...  91.7 us
    unnamed x1, local copies, waits for them, and re-layouts  1.88 us

profile of v4, /device:TPU:0, one launch (start us, length us, event | category | flops | bytes accessed | tf_op | source)
XLA Modules:
  0.0 93.5 jit_solution(17720232057798475105)
XLA Ops:
  0.0 91.7 %shard_map.64 = bf16[128,2048]{1,0:T(8,128)(2,1)} custom-call(bf16[128,2048]{1,0:T(8,128)(2,1)} %tok_ref.1, s32[8,128]{1,0:T(8,128)} %bitcast.2, f32[8,128]{1,0:T(8,128)} %bitcast.3, bf16[1,2048,1024]{2,1,0:T(8,128)(2,1)} %wg_hbm.1, bf16[1,2048,1024]{2,1,0:T(8,128)(2,1)} %wu_hbm.1, bf16[1,1024,2048]{2,1,0:T(8,128)(2,1)} %wd_hbm.1), custom_call_target="tpu_custom_call" | custom-call | tf_op jit(solution)/shard_map/pallas_call | solution.py:435
  91.7 1.9 %copy.8 = bf16[128,2048]{1,0:T(8,128)(2,1)} copy(bf16[128,2048]{1,0:T(8,128)(2,1)} %shard_map.64) | data formatting | bytes 1048576
